TPU v7x, 128 devices: a whole 4x4x4 slice. The times are simulated.
128 devices in a mesh: dp: 16 (over z, x_lo, core), mp: 8 (over x_hi, y).
Axes of the slice: x: 4 (x_hi: 2, x_lo: 2; x = x_hi * 2 + x_lo), y: 4, z: 4, core: 2. Of those that a mesh axis runs over, the one named last changes fastest.
Arguments:
- master: float32 [8192, 5120], P('dp', 'mp'), may hold values from -60 to 60
- moment_first: float32 [8192, 5120], P('dp', 'mp'), may hold values from -0.06 to 0.06
- moment_second: float32 [8192, 5120], P('dp', 'mp'), may hold values from 1e-05 to 0.001
- gradients: float32 [8192, 5120], P('dp', 'mp'), may hold values from -0.2 to 0.2
- step_count: int32 [1], replicated, may hold values from 1 to 10
- tensor_rows: int32 [24], replicated, may hold values from 1 to 1280, 8192 in all
- decay_mask: int32 [24], replicated, may hold values 0 or 1
Outputs:
- new_master: float32 [8192, 5120], P('dp', 'mp')
- new_first: float32 [8192, 5120], P('dp', 'mp')
- new_second: float32 [8192, 5120], P('dp', 'mp')
- compute_weights: bfloat16 [8192, 5120], P(None, 'mp')
Inputs may be any that keep to these rules, and one draw needn't show every extreme that they name: `tensor_rows`: the rows sum to 8192; the largest tensor has 1280 rows.
All inputs are finite; a program needn't handle non-finite values.
Results may differ from a plain program's by a relative error of at most 0.0004.
Values may be sent and summed in bfloat16 or wider, within the bound.
A program may use at most 128 MiB of HBM per device.

v0:
```python
import jax
import jax.numpy as jnp
from jax import lax
from jax.sharding import PartitionSpec as P

beta_first = 0.9
beta_second = 0.999
adam_epsilon = 1e-06
decay_rate = 0.3
learn_rate = 0.3
norm_epsilon = 1e-06


def copy_for_each(x, axis):
    size = lax.axis_size(axis)
    return lax.all_to_all(jnp.broadcast_to(x[None], (size, *x.shape)), axis, 0, 0, tiled=True)


def over_copies(x, axis):
    everything = copy_for_each(x, axis)
    return jnp.sum(everything, axis=0)


def together(arrays, axis):
    flat, at, gathered = (jnp.concatenate([a.reshape(-1) for a in arrays]), 0, [])
    subtotal = over_copies(flat, axis)
    for a in arrays:
        gathered.append(subtotal[at : at + a.size].reshape(a.shape))
        at += a.size
    return tuple(gathered)


def membership(first_row, count, offsets, tensor_rows):
    row_ids = first_row + jnp.arange(count, dtype=jnp.int32)
    inside = (row_ids[None, :] >= offsets[:, None]) & (
        row_ids[None, :] < (offsets + tensor_rows)[:, None]
    )
    return inside.astype(jnp.float32)


def local(master, moment_first, moment_second, gradients, step_count, tensor_rows, decay_mask):
    rows_dev = master.shape[0]
    steps = step_count[0].astype(jnp.float32)
    new_first = beta_first * moment_first + (1.0 - beta_first) * gradients
    new_second = beta_second * moment_second + (1.0 - beta_second) * gradients * gradients
    fix_first = 1.0 - jnp.power(jnp.float32(beta_first), steps)
    fix_second = 1.0 - jnp.power(jnp.float32(beta_second), steps)
    offsets = jnp.cumsum(tensor_rows) - tensor_rows
    first_row = lax.axis_index("dp") * rows_dev
    member = membership(first_row, rows_dev, offsets, tensor_rows)
    mask_rows = jnp.dot(decay_mask.astype(jnp.float32), member, precision=lax.Precision.HIGHEST)
    update = new_first / fix_first / (jnp.sqrt(new_second / fix_second) + adam_epsilon)
    update = update + decay_rate * mask_rows[:, None] * master
    weight_part = jnp.dot(member, jnp.sum(master * master, axis=1), precision=lax.Precision.HIGHEST)
    update_part = jnp.dot(member, jnp.sum(update * update, axis=1), precision=lax.Precision.HIGHEST)
    column_sums = together((weight_part, update_part), "mp")
    weight_sq, update_sq = together((column_sums[0], column_sums[1]), "dp")
    ratio = jnp.sqrt(weight_sq) / (jnp.sqrt(update_sq) + norm_epsilon)
    ratio_rows = jnp.dot(ratio, member, precision=lax.Precision.HIGHEST)
    new_master = master - learn_rate * ratio_rows[:, None] * update
    compute_weights = lax.all_gather(new_master.astype(jnp.bfloat16), "dp", axis=0, tiled=True)
    return (new_master, new_first, new_second, compute_weights)


def solution(mesh):
    placed = (P("dp", "mp"), P("dp", "mp"), P("dp", "mp"), P("dp", "mp"), P(), P(), P())
    return jax.shard_map(
        local,
        mesh=mesh,
        in_specs=placed,
        out_specs=(P("dp", "mp"), P("dp", "mp"), P("dp", "mp"), P(None, "mp")),
        check_vma=False,
    )
```

profile of v0, /device:TPU:1, one launch (start us, length us, event | category | flops | bytes accessed | tf_op | source)
XLA Modules:
  0.0 118.2 jit_solution(8679923997820081381)
XLA Ops:
  7.2 0.0 all-gather.2.cloned.1.call-start
  8.0 0.7 copy.14
  8.7 0.1 reduce.2
  8.9 0.7 sub.18
  9.5 0.1 compare_and_fusion
  9.6 0.8 fusion.2
  10.4 0.0 copy-start
  10.4 5.1 %multiply_reduce_fusion = (f32[512]{0:T(512)S(1)}, f32[512,640]{1,0:T(8,128)S(1)}, f32[512,640]{1,0:T(8,128)}, f32[512,640]{1,0:T(8,128)}, f32[512]{0:T(512)S(1)}) fusion(f32[512,640]{1,0:T(8,128)} %param.7, f32[512]{0:T(512)S(1)} %broadcast_multiply_fusion.1, f32[]{:T(128)} %bitcast.4, f32[]{:T(128)} %bitcast.3, f32[512,640]{1,0:T(8,128)} %param.10, ...), kind=kLoop, calls=%fused_computation.3 | loop fusion | flops 5569536 | bytes 9181192 | tf_op jit(solution)/shard_map/reduce_sum | solution.py:55
  15.5 0.1 convolution_bitcast_fusion
  15.6 0.1 convolution_bitcast_fusion.1
  15.7 0.1 pad_maximum_fusion
  15.8 13.8 %all_to_all.12 = f32[8,1,48]{2,1,0:T(1,128)S(1)} all-to-all(f32[8,1,48]{2,1,0:T(1,128)S(1)} %broadcast_in_dim.4), channel_id=1, replica_groups=mesh['dp'=16,'mp'=8] {'mp'}, dimensions={0} | all-to-all | bytes 3072 | tf_op jit(solution)/shard_map/all_to_all | solution.py:16
  29.7 12.8 %all_to_all.13 = f32[16,1,48]{2,1,0:T(1,128)S(1)} all-to-all(f32[16,1,48]{2,1,0:T(1,128)S(1)} %broadcast_in_dim.5), channel_id=1, replica_groups=mesh['dp'=16,'mp'=8] {'dp'}, dimensions={0} | all-to-all | bytes 6144 | tf_op jit(solution)/shard_map/all_to_all | solution.py:16
  42.5 0.2 fusion.3
  42.7 0.0 copy-done
  42.7 1.5 %fusion.7 = (bf16[512,640]{1,0:T(8,128)(2,1)}, f32[512,640]{1,0:T(8,128)}) fusion(f32[512,640]{1,0:T(8,128)S(1)} %copy-done, f32[512,640]{1,0:T(8,128)S(1)} %get-tuple-element.7, f32[512]{0:T(512)S(1)} %broadcast_multiply_fusion), kind=kLoop, calls=%fused_computation.21 | loop fusion | flops 983040 | bytes 4589568 | tf_op jit(solution)/shard_map/convert_element_type | solution.py:61
  44.2 0.0 all-gather.2.cloned.1.call-update
  44.2 58.2 %all-gather.2.cloned.1.call-done = bf16[8192,640]{1,0:T(8,128)(2,1)} async-done(((bf16[512,640]{1,0:T(8,128)(2,1)}), bf16[8192,640]{1,0:T(8,128)(2,1)}) %all-gather.2.cloned.1.call-update) | async-done | bytes 10485776 | tf_op jit(solution)/shard_map/all_gather | solution.py:61
  102.4 9.0 %copy.19 = bf16[8192,640]{1,0:T(8,128)(2,1)} copy(bf16[8192,640]{1,0:T(8,128)(2,1)} %all-gather.2.cloned.1.call-done) | data formatting | bytes 20971520
  (8 shorter events, 0.1 us)
Async XLA Ops:
  7.2 95.2 %all-gather.2.cloned.1.call-start = ((), (), s32[]{:S(2)}) async-start(), calls=%async_computation.2 | async-start | bytes 11141120 | tf_op jit(solution)/shard_map/all_gather | solution.py:61
  10.4 32.3 %copy-start = (f32[512,640]{1,0:T(8,128)S(1)}, f32[512,640]{1,0:T(8,128)}, u32[]{:S(2)}) copy-start(f32[512,640]{1,0:T(8,128)} %param.7) | copy-start | bytes 3932164
Sparse Core Ops, SparseCore 0:
  44.3 58.0 all-gather.1
where the time goes:
time: 118 us
  waiting for transfers between devices  58.2 us (49%)
  blocking collectives  26.6 us (23%)
  between operations  14.8 us (13%)
  local copies, waits for them, and re-layouts  9.72 us (8%)
  other arithmetic  7.61 us (6%)
  matrix products  1.26 us (1%)
    all_gather x1, waiting for transfers between devices, local(): lax.all_gather(new_master.astype(jnp.bfloat16), 'dp', axis=0, tiled=True)  58.2 us
    all_to_all x2, blocking collectives, copy_for_each(): lax.all_to_all(jnp.broadcast_to(x[None], (size, *x.shape)), axis, 0, 0, t...  26.6 us
    unnamed x3, local copies, waits for them, and re-layouts  8.97 us
    reduce_sum x1, other arithmetic, local(): jnp.sum(update * update, axis=1)  5.08 us
  transfers between devices with their start and end apart: 1, of which 1 were waited for; matrix products, arithmetic and copies ran while one was open for 0% of the time, Pallas kernels for 0%

commit v1 on v0

--- a/solution.py
+++ b/solution.py
@@ -58,7 +58,12 @@
     ratio = jnp.sqrt(weight_sq) / (jnp.sqrt(update_sq) + norm_epsilon)
     ratio_rows = jnp.dot(ratio, member, precision=lax.Precision.HIGHEST)
     new_master = master - learn_rate * ratio_rows[:, None] * update
-    compute_weights = lax.all_gather(new_master.astype(jnp.bfloat16), "dp", axis=0, tiled=True)
+    compute_weights = jnp.concatenate(
+        lax.all_to_all(
+            jnp.stack(lax.axis_size("dp") * [new_master.astype(jnp.bfloat16)]), "dp", 0, 0
+        ),
+        axis=0,
+    )
     return (new_master, new_first, new_second, compute_weights)
 
 

time: 118 us -> 168 us (1.42)
  blocking collectives: 26.6 us -> 147 us
  waiting for transfers between devices: 58.2 us -> 0 us
  between operations: 14.8 us -> 1.4 us
    all_to_all x0 -> x1, blocking collectives: none -> 120 us  [local(): lax.all_to_all(jnp.stack(lax.axis_size('dp') * [new_master.astype(jnp.bfl...]
    all_gather x1 -> x0, waiting for transfers between devices: 58.2 us -> none  [local(): lax.all_gather(new_master.astype(jnp.bfloat16), 'dp', axis=0, tiled=True)]
  transfers between devices with their start and end apart: 1 -> 0, of which waited for: 1 -> 0; matrix products, arithmetic and copies ran while one was open for 0% -> 0% of each run, Pallas kernels for 0% -> 0%
where the time goes in v1:
time: 168 us
  blocking collectives  147 us (88%)
  local copies, waits for them, and re-layouts  10.9 us (6%)
  other arithmetic  7.4 us (4%)
    all_to_all x1, blocking collectives, local(): lax.all_to_all(jnp.stack(lax.axis_size('dp') * [new_master.astype(jnp.bfl...  120 us
    all_to_all x2, blocking collectives, copy_for_each(): lax.all_to_all(jnp.broadcast_to(x[None], (size, *x.shape)), axis, 0, 0, t...  26.6 us
    unnamed x3, local copies, waits for them, and re-layouts  8.97 us
    reduce_sum x1, other arithmetic, local(): jnp.sum(update * update, axis=1)  5.08 us

profile of v1, /device:TPU:1, one launch (start us, length us, event | category | flops | bytes accessed | tf_op | source)
XLA Modules:
  0.0 168.0 jit_solution(8923153106042986510)
XLA Ops:
  1.4 0.7 copy.14
  2.2 0.1 reduce.2
  2.3 0.7 sub.18
  2.9 0.1 compare_and_fusion
  3.0 0.8 fusion.2
  3.8 0.0 copy-start
  3.8 5.1 %multiply_reduce_fusion = (f32[512]{0:T(512)S(1)}, f32[512,640]{1,0:T(8,128)S(1)}, f32[512,640]{1,0:T(8,128)}, f32[512,640]{1,0:T(8,128)}, f32[512]{0:T(512)S(1)}) fusion(f32[512,640]{1,0:T(8,128)} %param.7, f32[512]{0:T(512)S(1)} %broadcast_multiply_fusion.1, f32[]{:T(128)} %bitcast.4, f32[]{:T(128)} %bitcast.3, f32[512,640]{1,0:T(8,128)} %param.10, ...), kind=kLoop, calls=%fused_computation.3 | loop fusion | flops 5569536 | bytes 9181192 | tf_op jit(solution)/shard_map/reduce_sum | solution.py:55
  8.9 0.1 convolution_bitcast_fusion
  9.0 0.1 convolution_bitcast_fusion.1
  9.2 0.1 pad_maximum_fusion
  9.3 13.8 %all_to_all.17 = f32[8,1,48]{2,1,0:T(1,128)S(1)} all-to-all(f32[8,1,48]{2,1,0:T(1,128)S(1)} %broadcast_in_dim.4), channel_id=1, replica_groups=mesh['dp'=16,'mp'=8] {'mp'}, dimensions={0} | all-to-all | bytes 3072 | tf_op jit(solution)/shard_map/all_to_all | solution.py:16
  23.1 12.8 %all_to_all.18 = f32[16,1,48]{2,1,0:T(1,128)S(1)} all-to-all(f32[16,1,48]{2,1,0:T(1,128)S(1)} %broadcast_in_dim.5), channel_id=1, replica_groups=mesh['dp'=16,'mp'=8] {'dp'}, dimensions={0} | all-to-all | bytes 6144 | tf_op jit(solution)/shard_map/all_to_all | solution.py:16
  35.9 0.2 fusion.3
  36.1 0.0 copy-done
  36.1 1.3 fusion.7
  37.4 1.2 stack.2
  38.6 120.5 %all_to_all.19 = bf16[16,512,640]{2,1,0:T(8,128)(2,1)} all-to-all(bf16[16,512,640]{2,1,0:T(8,128)(2,1)S(1)} %stack.2), channel_id=1, replica_groups=mesh['dp'=16,'mp'=8] {'dp'}, dimensions={0} | all-to-all | bytes 20971520 | tf_op jit(solution)/shard_map/all_to_all | solution.py:62
  159.1 9.0 %copy.19 = bf16[8192,640]{1,0:T(8,128)(2,1)} copy(bf16[8192,640]{1,0:T(8,128)(2,1)} %bitcast.26) | data formatting | bytes 20971520
  (8 shorter events, 0.1 us)
Async XLA Ops:
  3.8 32.3 %copy-start = (f32[512,640]{1,0:T(8,128)S(1)}, f32[512,640]{1,0:T(8,128)}, u32[]{:S(2)}) copy-start(f32[512,640]{1,0:T(8,128)} %param.7) | copy-start | bytes 3932164
